TPU v7x, 128 devices: a whole 4x4x4 slice. The times are simulated.
128 devices in a mesh: dp: 1, hp: 16 (over z, y), cp: 8 (over x, core).
Axes of the slice: x: 4, y: 4, z: 4, core: 2. Of those that a mesh axis runs over, the one named last changes fastest.
Arguments:
- latent: bfloat16 [96, 16, 48, 512], P(('dp', 'cp'), 'hp')
- conv_w: bfloat16 [4, 3, 3, 3, 512, 512], replicated
- conv_b: float32 [4, 512], replicated
- gn_gamma: float32 [4, 512], replicated
- gn_beta: float32 [4, 512], replicated
Outputs:
- output: bfloat16 [96, 16, 48, 512], P(('dp', 'cp'), 'hp')
All inputs are finite; a program needn't handle non-finite values.
Results may differ from a plain program's by a relative error of at most 0.00972573.
Values are sent between devices in bfloat16 or wider.
A program may use at most 1 GiB of HBM per device.

v0:
```python
import functools

import jax
import jax.numpy as jnp
from jax import lax
from jax.experimental import pallas as pl
from jax.experimental.pallas import tpu as pltpu
from jax.sharding import PartitionSpec as P

GROUPS = 32
EPS = 1e-6
LAYERS = 4
MESH = pl.DeviceIdType.MESH
CHUNK = 3


def lane_sums(y, lane):
    for s in (1, 4):
        place = (lane // s) & 3
        total = y
        for d in (-3, -2, -1, 1, 2, 3):
            inside = jnp.logical_and(place + d >= 0, place + d <= 3)
            total = total + jnp.where(inside, pltpu.roll(y, (-d * s) % 128, 1), 0.0)
        y = total
    return y


def tree_sum(terms):
    while len(terms) > 1:
        terms = [a + b for a, b in zip(terms[::2], terms[1::2])] + terms[len(terms) & ~1 :]
    return terms[0]


def decode_kernel(n_hp, n_cp, total_count, lat_ref, w_ref, b_ref, g_ref, be_ref, o_ref,
                  wbuf, raw, act, xres, small, params, ssum, st8, coef, msg, peers,
                  w_sem, lat_sem, small_sem, send_sem, recv_sem, msg_send, msg_recv):
    frames, width, channels = xres.shape
    n_chunks = frames // CHUNK
    hp = lax.axis_index("hp")
    cp = lax.axis_index("cp")
    has_up = hp > 0
    has_down = hp < n_hp - 1
    has_next = cp < n_cp - 1
    has_prev = cp > 0
    odd = lax.rem(cp, 2) == 1

    slab_order = [(k, 1) for k in range(3)] + [(k, di) for di in (0, 2) for k in range(3)]

    def weight_copy(layer, slot, k, di):
        slab = k * 3 + di
        return pltpu.make_async_copy(w_ref.at[layer, slab], wbuf.at[slot, slab], w_sem.at[slot, slab])

    def start_weights(layer, slot):
        for k, di in slab_order:
            weight_copy(layer, slot, k, di).start()

    lat_copies = [pltpu.make_async_copy(lat_ref, raw.at[0, 1, pl.ds(2, frames)], lat_sem.at[0]),
                  pltpu.make_async_copy(lat_ref, xres, lat_sem.at[1])]
    small_copies = [pltpu.make_async_copy(ref, small.at[i], small_sem.at[i]) for i, ref in enumerate((b_ref, g_ref, be_ref))]
    for copy in lat_copies + small_copies:
        copy.start()

    def others(visit):
        @pl.loop(0, n_hp)
        def _(i):
            for j in range(n_cp):
                target = {"hp": lax.rem(hp + n_hp // 2 + i, n_hp), "cp": lax.rem(cp + n_cp // 2 + j, n_cp)}
                if j == n_cp // 2:
                    pl.when(i != n_hp // 2)(functools.partial(visit, target))
                else:
                    visit(target)

    barrier = pltpu.get_barrier_semaphore()
    with jax.named_scope("entry_signals"):
        others(lambda target: pl.semaphore_signal(barrier, inc=1, device_id=target, device_id_type=MESH))

    def row_copy(slot, c, to_down):
        span = pl.ds(2 + c * CHUNK, CHUNK)
        row = 0 if to_down else 2
        return pltpu.make_async_remote_copy(
            src_ref=raw.at[slot, 1, span], dst_ref=raw.at[slot, row, span],
            send_sem=send_sem.at[slot, row, c], recv_sem=recv_sem.at[slot, row, c],
            device_id={"hp": hp + (1 if to_down else -1)}, device_id_type=MESH)

    def time_copy(slot, dh):
        row = dh if dh is None else (0 if dh == 1 else 2)
        row = 1 if dh == 0 else row
        return pltpu.make_async_remote_copy(
            src_ref=raw.at[slot, 1, pl.ds(frames, 2)], dst_ref=raw.at[slot, row, pl.ds(0, 2)],
            send_sem=send_sem.at[slot, row, n_chunks], recv_sem=recv_sem.at[slot, row, n_chunks],
            device_id={"hp": hp + dh, "cp": cp + 1}, device_id_type=MESH)

    def start_rows(slot, c):
        @pl.when(has_up)
        def _():
            row_copy(slot, c, False).start()

        @pl.when(has_down)
        def _():
            row_copy(slot, c, True).start()

    def start_times(slot):
        @pl.when(has_next)
        def _():
            time_copy(slot, 0).start()

        @pl.when(jnp.logical_and(has_next, has_up))
        def _():
            time_copy(slot, -1).start()

        @pl.when(jnp.logical_and(has_next, has_down))
        def _():
            time_copy(slot, 1).start()

    def wait_sends(slot):
        for c in range(n_chunks):
            @pl.when(has_up)
            def _():
                row_copy(slot, c, False).wait_send()

            @pl.when(has_down)
            def _():
                row_copy(slot, c, True).wait_send()

        @pl.when(has_next)
        def _():
            time_copy(slot, 0).wait_send()

        @pl.when(jnp.logical_and(has_next, has_up))
        def _():
            time_copy(slot, -1).wait_send()

        @pl.when(jnp.logical_and(has_next, has_down))
        def _():
            time_copy(slot, 1).wait_send()

    for row, ok in ((0, has_up), (2, has_down)):
        @pl.when(jnp.logical_not(ok))
        def _():
            @pl.loop(0, frames + 2)
            def _(f):
                for slot in range(2):
                    raw[slot, row, f] = jnp.zeros((width, channels), jnp.bfloat16)

    @pl.when(jnp.logical_not(has_prev))
    def _():
        for slot in range(2):
            for row in range(3):
                for f in range(2):
                    raw[slot, row, f] = jnp.zeros((width, channels), jnp.bfloat16)

    with jax.named_scope("lat_wait"):
        for copy in lat_copies:
            copy.wait()
    start_weights(0, 0)

    def fold(v):
        return jnp.sum(v.reshape(-1, 8, v.shape[-1]), axis=0)

    ssum[...] = jnp.zeros_like(ssum)

    @pl.loop(0, frames)
    def _(f):
        v = xres[f].astype(jnp.float32)
        ssum[0] += fold(v)
        ssum[1] += fold(v * v)

    lane = lax.broadcasted_iota(jnp.int32, (8, 128), 1)
    sub = lax.broadcasted_iota(jnp.int32, (8, 128), 0)
    pick = (lane & 15) == sub

    me = hp * n_cp + cp

    def send_sums(layer):
        for s in range(2):
            for i in range(4):
                st8[s * 4 + i : s * 4 + i + 1, :] = jnp.sum(ssum[s, :, i * 128 : (i + 1) * 128], axis=0, keepdims=True)
        mine = jnp.where(pick, lane_sums(st8[...], lane), 0.0)
        msg[layer] = jnp.sum(mine, axis=0, keepdims=True)
        peers[layer, me] = msg[layer]
        others(lambda target: pltpu.make_async_remote_copy(
            src_ref=msg.at[layer], dst_ref=peers.at[layer, me], send_sem=msg_send.at[layer], recv_sem=msg_recv.at[layer],
            device_id=target, device_id_type=MESH).start())

    def statistics(layer):
        rest = peers.at[layer, pl.ds(0, n_hp * n_cp - 1)]
        pltpu.make_async_copy(rest, rest, msg_recv.at[layer]).wait()
        pltpu.make_async_copy(rest, rest, msg_send.at[layer]).wait()
        total = tree_sum([peers[layer, i] for i in range(n_hp * n_cp)])
        st8[...] = lane_sums(jnp.where(pick, jnp.broadcast_to(total, (8, 128)), 0.0), lane)
        mean = st8[0:4, :] * (1.0 / total_count)
        var = st8[4:8, :] * (1.0 / total_count) - mean * mean
        inv = lax.rsqrt(var + EPS)
        st8[0:4, :] = inv
        st8[4:8, :] = mean * inv
        for i in range(4):
            lanes = slice(i * 128, (i + 1) * 128)
            gamma = 0.5 * params[1, layer, :, lanes]
            scale = gamma * st8[i : i + 1, :]
            shift = 0.5 * params[2, layer, :, lanes] - st8[4 + i : 5 + i, :] * gamma
            for row, ok in ((0, has_up), (1, None), (2, has_down)):
                coef[row, 0:1, lanes] = scale if ok is None else jnp.where(ok, scale, 0.0)
                coef[row, 1:2, lanes] = shift if ok is None else jnp.where(ok, shift, 0.0)

    first_frame = jnp.where(has_prev, 0, 2)
    col = lax.broadcasted_iota(jnp.int32, (width, channels), 0)

    def activate(slot, row, f):
        v = raw[slot, row, jnp.maximum(f, first_frame)].astype(jnp.float32)
        u = v * coef[row, 0:1, :] + coef[row, 1:2, :]
        y = u * jnp.tanh(u) + u
        left = jnp.where(col == 0, 0.0, pltpu.roll(y, 1, 0))
        right = jnp.where(col == width - 1, 0.0, pltpu.roll(y, width - 1, 0))
        for dj, v in enumerate((left, y, right)):
            act[row, f, :, dj * channels : (dj + 1) * channels] = v.astype(jnp.bfloat16)

    def halo_wait(slot, c, row):
        ok = has_up if row == 0 else has_down
        if c == 0:
            @pl.when(jnp.logical_and(ok, has_prev))
            def _():
                time_copy(slot, 1 if row == 0 else -1).wait_recv()

        @pl.when(ok)
        def _():
            row_copy(slot, c, row == 0).wait_recv()

    def conv_chunk(slot, c):
        new = range(c * CHUNK + 2 if c else 0, c * CHUNK + 5)
        for row in (0, 2):
            halo_wait(slot, c, row)
        for f in new:
            activate(slot, 1, f)
        side = [functools.partial(activate, slot, row, f) for f in new for row in (0, 2)]
        total = None
        for n, row in enumerate((1, 0, 2)):
            for k in range(3):
                lhs = act[row, c * CHUNK + k : c * CHUNK + k + CHUNK].reshape(CHUNK * width, 3 * channels)
                part = jnp.dot(lhs, wbuf[slot, k * 3 + row], preferred_element_type=jnp.float32)
                total = part if total is None else total + part
                if n == 0:
                    for work in side[len(side) * k // 3 : len(side) * (k + 1) // 3]:
                        work()
        return total.reshape(CHUNK, width, channels)

    def finish(layer, other, c, y):
        second = lax.rem(layer, 2) == 1
        for f in range(c * CHUNK, (c + 1) * CHUNK):
            h = (y[f - c * CHUNK] + params[0, layer]).astype(jnp.bfloat16).astype(jnp.float32)
            x = xres[f].astype(jnp.float32)
            out = (h + jnp.where(second, x, 0.0)).astype(jnp.bfloat16)
            raw[other, 1, 2 + f] = out
            o_ref[f] = out
            out = out.astype(jnp.float32)
            xres[f] = jnp.where(second, out, x).astype(jnp.bfloat16)
            ssum[0] += fold(out)
            ssum[1] += fold(out * out)

    for copy in small_copies:
        copy.wait()
    for i in range(3):
        for layer in range(LAYERS):
            params[i, layer] = small[i, layer : layer + 1, :]
    with jax.named_scope("entry_wait"):
        pl.semaphore_wait(barrier, n_hp * n_cp - 1)
    with jax.named_scope("send_sums"):
        send_sums(0)
    start_times(0)
    for c in range(n_chunks):
        start_rows(0, c)

    def layer_body(layer, _):
        slot = lax.rem(layer, 2)
        other = 1 - slot
        more = layer < LAYERS - 1

        @pl.when(more)
        def _():
            start_weights(layer + 1, other)

        with jax.named_scope("statistics"):
            statistics(layer)

        with jax.named_scope("w_wait"):
            @pl.when(has_prev)
            def _():
                time_copy(slot, 0).wait_recv()

            for k, di in slab_order:
                weight_copy(layer, slot, k, di).wait()

        ssum[...] = jnp.zeros_like(ssum)
        for c in range(n_chunks):
            with jax.named_scope(f"chunk{c}"):
                finish(layer, other, c, conv_chunk(slot, c))
            if c < n_chunks - 1:
                @pl.when(more if c < 2 else jnp.logical_and(more, odd))
                def _():
                    start_rows(other, c)

        with jax.named_scope("send_wait"):
            wait_sends(slot)
        @pl.when(more)
        def _():
            with jax.named_scope("send_sums"):
                send_sums(layer + 1)
            with jax.named_scope("send_rest"):
                start_times(other)

                @pl.when(jnp.logical_not(odd))
                def _():
                    start_rows(other, n_chunks - 2)

                start_rows(other, n_chunks - 1)

        return 0

    lax.fori_loop(0, LAYERS, layer_body, 0)


def solution(mesh):
    n_hp, n_cp = mesh.shape["hp"], mesh.shape["cp"]

    def local_decode(lat, conv_w, conv_b, gn_gamma, gn_beta):
        frames, rows, width, channels = lat.shape
        n_chunks = frames // CHUNK
        total_count = float(frames * n_cp * rows * n_hp * width * (channels // GROUPS))
        hbm_spec = pl.BlockSpec(memory_space=pltpu.HBM)
        bf16, f32 = jnp.bfloat16, jnp.float32
        flops = LAYERS * 2 * frames * width * 27 * channels * channels
        out = pl.pallas_call(
            functools.partial(decode_kernel, n_hp, n_cp, total_count),
            out_shape=jax.ShapeDtypeStruct((frames, width, channels), bf16),
            in_specs=[hbm_spec] * 5,
            out_specs=pl.BlockSpec(memory_space=pltpu.VMEM),
            scratch_shapes=[
                pltpu.VMEM((2, 9, 3 * channels, channels), bf16),
                pltpu.VMEM((2, 3, frames + 2, width, channels), bf16),
                pltpu.VMEM((3, frames + 2, width, 3 * channels), bf16),
                pltpu.VMEM((frames, width, channels), bf16),
                pltpu.VMEM((3, LAYERS, channels), f32),
                pltpu.VMEM((3, LAYERS, 1, channels), f32),
                pltpu.VMEM((2, 8, channels), f32),
                pltpu.VMEM((8, 128), f32),
                pltpu.VMEM((3, 8, channels), f32),
                pltpu.VMEM((LAYERS, 1, 128), f32),
                pltpu.VMEM((LAYERS, n_hp * n_cp, 1, 128), f32),
                pltpu.SemaphoreType.DMA((2, 9)),
                pltpu.SemaphoreType.DMA((2,)),
                pltpu.SemaphoreType.DMA((3,)),
                pltpu.SemaphoreType.DMA((2, 3, n_chunks + 1)),
                pltpu.SemaphoreType.DMA((2, 3, n_chunks + 1)),
                pltpu.SemaphoreType.DMA((LAYERS,)),
                pltpu.SemaphoreType.DMA((LAYERS,)),
            ],
            compiler_params=pltpu.CompilerParams(
                collective_id=0, has_side_effects=True, vmem_limit_bytes=46 * 1024 * 1024),
            cost_estimate=pl.CostEstimate(flops=flops, bytes_accessed=conv_w.size * 2, transcendentals=0),
        )(*(pltpu.with_memory_space_constraint(v, pltpu.HBM) for v in (
            lat.reshape(frames, width, channels), conv_w.reshape(LAYERS, 9, 3 * channels, channels),
            conv_b, gn_gamma, gn_beta)))
        return out.reshape(lat.shape)

    video_spec = P(("dp", "cp"), "hp", None, None)
    return jax.shard_map(local_decode, mesh=mesh, in_specs=(video_spec, P(), P(), P(), P()), out_specs=video_spec, check_vma=False)
```

profile of v0, /device:TPU:2, one launch (start us, length us, event | category | flops | bytes accessed | tf_op | source)
XLA Modules:
  0.0 91.6 jit_solution(1216236880140135424)
XLA Ops:
  0.0 90.8 %shard_map.55 = bf16[12,48,512]{2,1,0:T(8,128)(2,1)S(1)} custom-call(bf16[12,48,512]{2,1,0:T(8,128)(2,1)} %bitcast.7, bf16[4,9,1536,512]{3,2,1,0:T(8,128)(2,1)} %bitcast.6, f32[4,512]{1,0:T(4,128)} %b_ref.1, f32[4,512]{1,0:T(4,128)} %g_ref.1, f32[4,512]{1,0:T(4,128)} %be_ref.1), custom_call_target="tpu_custom_call" | custom-call | flops 32614907904 | bytes 56623104 | tf_op jit(solution)/shard_map/pallas_call | solution.py:331
  90.8 0.8 copy.8
where the time goes:
time: 91.9 us; the launch traced here: 91.6 us
  Pallas kernels  90.8 us (99%)
    pallas_call x1, Pallas kernels, local_decode(): pl.pallas_call(functools.partial(decode_kernel, n_hp, n_cp, total_count),...  90.8 us

commit v1 on v0

--- a/solution.py
+++ b/solution.py
@@ -42,7 +42,6 @@
     has_down = hp < n_hp - 1
     has_next = cp < n_cp - 1
     has_prev = cp > 0
-    odd = lax.rem(cp, 2) == 1
 
     slab_order = [(k, 1) for k in range(3)] + [(k, di) for di in (0, 2) for k in range(3)]
 
@@ -294,7 +293,7 @@
             with jax.named_scope(f"chunk{c}"):
                 finish(layer, other, c, conv_chunk(slot, c))
             if c < n_chunks - 1:
-                @pl.when(more if c < 2 else jnp.logical_and(more, odd))
+                @pl.when(more)
                 def _():
                     start_rows(other, c)
 
@@ -306,10 +305,6 @@
                 send_sums(layer + 1)
             with jax.named_scope("send_rest"):
                 start_times(other)
-
-                @pl.when(jnp.logical_not(odd))
-                def _():
-                    start_rows(other, n_chunks - 2)
 
                 start_rows(other, n_chunks - 1)
 

time: 91.9 us -> 97.7 us (1.063)
  Pallas kernels: 90.8 us -> 96.7 us
    pallas_call x1, Pallas kernels: 90.8 us -> 96.7 us  [local_decode(): pl.pallas_call(functools.partial(decode_kernel, n_hp, n_cp, total_count),...]
where the time goes in v1:
time: 97.7 us; the launch traced here: 97.5 us
  Pallas kernels  96.7 us (99%)
    pallas_call x1, Pallas kernels, local_decode(): pl.pallas_call(functools.partial(decode_kernel, n_hp, n_cp, total_count),...  96.7 us

profile of v1, /device:TPU:2, one launch (start us, length us, event | category | flops | bytes accessed | tf_op | source)
XLA Modules:
  0.0 97.5 jit_solution(1359039104118905343)
XLA Ops:
  0.0 96.7 %shard_map.55 = bf16[12,48,512]{2,1,0:T(8,128)(2,1)S(1)} custom-call(bf16[12,48,512]{2,1,0:T(8,128)(2,1)} %bitcast.7, bf16[4,9,1536,512]{3,2,1,0:T(8,128)(2,1)} %bitcast.6, f32[4,512]{1,0:T(4,128)} %b_ref.1, f32[4,512]{1,0:T(4,128)} %g_ref.1, f32[4,512]{1,0:T(4,128)} %be_ref.1), custom_call_target="tpu_custom_call" | custom-call | flops 32614907904 | bytes 56623104 | tf_op jit(solution)/shard_map/pallas_call | solution.py:326
  96.7 0.8 copy.8
